TPU v7x, 32 devices: a whole 2x2x4 slice. The times are simulated.
32 devices in a mesh: blk: 16 (over z, y, x), ga: 2 (over core).
Axes of the slice: x: 2, y: 2, z: 4, core: 2. Of those that a mesh axis runs over, the one named last changes fastest.
Arguments:
- pair_elements: bfloat16 [4096, 16384], P('ga', 'blk'), may hold values from -6 to 6
- screening: bfloat16 [4096, 4096], P('ga', 'blk'), may hold values from -0.09375 to 0.09375
- energies: float32 [256], replicated, may hold values from 0.5 to 3
- frequencies: float32 [8], replicated, may hold values from 0.3 to 3
- qp_index: int32 [32], replicated, may hold values from 0 to 255
- occupied: int32 [256], replicated, may hold values 0 or 1
Outputs:
- self_energy: float32 [2, 8, 32, 32], replicated
All inputs are finite; a program needn't handle non-finite values.
Results may differ from a plain program's by a relative error of at most 0.0003.
Values may be sent and summed in bfloat16 or wider, within the bound.
A program may use at most 128 MiB of HBM per device.

v0:
```python
import jax
import jax.numpy as jnp
from jax import lax
from jax.sharding import PartitionSpec as P

STATES = 32
NG = 4096


def band_weights(energies, frequencies, qp_index, occupied, offset, band_count):
    level_count = energies.shape[0]
    position = jnp.arange(level_count, dtype=jnp.int32)
    signed = jnp.where(occupied == 1, -energies, energies)
    onehot = (qp_index[:, None] == position[None, :]).astype(jnp.float32)
    state_level = jnp.sum(onehot * signed[None, :], axis=1)
    band_level = lax.dynamic_slice_in_dim(signed, offset, band_count, 0)
    detuning = state_level[:, None] - band_level[None, :]
    imag_freq = frequencies[:, None, None]
    modulus = detuning[None] ** 2 + imag_freq**2
    return (detuning[None] / modulus, -imag_freq / modulus)


def window_sigma(elements, screened, weight_real, weight_imag, band_count):
    row_count = elements.shape[0]
    local_elems = elements.astype(jnp.float32).reshape(row_count, band_count, 2, STATES)
    image_cols = screened.reshape(row_count, band_count, 2, STATES)
    intersection = jnp.einsum(
        "gnpi,gnqj->npiqj", local_elems, image_cols, precision=lax.Precision.HIGHEST
    )
    intersection_real = intersection[:, 0, :, 0, :] + intersection[:, 1, :, 1, :]
    intersection_imag = intersection[:, 0, :, 1, :] - intersection[:, 1, :, 0, :]
    sigma_real = jnp.einsum(
        "kin,nij->kij", weight_real, intersection_real, precision=lax.Precision.HIGHEST
    ) - jnp.einsum("kin,nij->kij", weight_imag, intersection_imag, precision=lax.Precision.HIGHEST)
    sigma_imag = jnp.einsum(
        "kin,nij->kij", weight_real, intersection_imag, precision=lax.Precision.HIGHEST
    ) + jnp.einsum("kin,nij->kij", weight_imag, intersection_real, precision=lax.Precision.HIGHEST)
    return jnp.stack([sigma_real, sigma_imag]) / NG


def shards(pair_elements, screening, energies, frequencies, qp_index, occupied):
    col_count = pair_elements.shape[1]
    band_count = col_count // (2 * STATES)
    gathered = lax.all_gather(pair_elements, "ga", axis=0, tiled=True)
    screened = jnp.dot(
        lax.all_gather(screening, "blk", axis=1, tiled=True),
        gathered,
        preferred_element_type=jnp.float32,
    )
    band_start = lax.axis_index("blk") * band_count
    weight_real, weight_imag = band_weights(
        energies, frequencies, qp_index, occupied, band_start, band_count
    )
    partial_value = window_sigma(pair_elements, screened, weight_real, weight_imag, band_count)
    return lax.psum(partial_value, ("blk", "ga"))


def solution(mesh):
    placed = (P("ga", "blk"), P("ga", "blk"), P(), P(), P(), P())
    return jax.shard_map(shards, mesh=mesh, in_specs=placed, out_specs=P(), check_vma=False)
```

profile of v0, /device:TPU:0, one launch (start us, length us, event | category | flops | bytes accessed | tf_op | source)
XLA Modules:
  0.0 443.0 jit_solution(11646669424119894896)
XLA Ops:
  6.5 0.0 all-gather.5.cloned.1.call-start
  6.6 0.7 all-gather.5.cloned.1.call-update
  7.3 0.0 all-gather.3.cloned.1.call-start
  7.3 0.7 all-gather.3.cloned.1.call-update
  8.0 0.0 all-reduce.2.cloned.1.call-start
  8.1 6.6 %copy.19 = bf16[2048,1024]{0,1:T(8,128)(2,1)} copy(bf16[2048,1024]{1,0:T(8,128)(2,1)} %param.6) | data formatting | bytes 8388608 | tf_op args[0]
  14.7 0.1 dynamic_slice.3
  14.8 0.2 select_reduce_fusion
  14.9 0.1 broadcast_subtract_fusion
  15.0 16.5 %all-gather.5.cloned.1.call-done = bf16[4096,1024]{1,0:T(8,128)(2,1)} async-done(((bf16[2048,1024]{1,0:T(8,128)(2,1)}), bf16[4096,1024]{1,0:T(8,128)(2,1)}) %all-gather.5.cloned.1.call-update) | async-done | bytes 8388624 | tf_op jit(solution)/shard_map/all_gather | solution.py:44
  31.5 238.5 %all-gather.3.cloned.1.call-done = bf16[2048,4096]{1,0:T(8,128)(2,1)} async-done(((bf16[2048,256]{1,0:T(8,128)(2,1)}), bf16[2048,4096]{1,0:T(8,128)(2,1)}) %all-gather.3.cloned.1.call-update) | async-done | bytes 16777232 | tf_op jit(solution)/shard_map/all_gather | solution.py:46
  270.0 24.3 %fusion.20 = f32[2048,1024]{0,1:T(8,128)} fusion(bf16[2048,4096]{1,0:T(8,128)(2,1)} %all-gather.3.cloned.1.call-done, bf16[4096,1024]{1,0:T(8,128)(2,1)} %all-gather.5.cloned.1.call-done), kind=kOutput, calls=%fused_computation.32 | convolution fusion | flops 17179869184 | bytes 33554432 | tf_op jit(solution)/shard_map/dot_general | solution.py:45
  294.3 12.7 %convolution_bitcast_fusion = f32[16,2,32,2,32]{2,4,1,3,0:T(8,128)S(1)} fusion(f32[2048,16,2,32,1]{0,3,4,2,1:T(8,128)} %bitcast.33, bf16[2048,16,2,32,1]{0,3,2,4,1:T(8,128)(2,1)S(1)} %bitcast.32), kind=kOutput, calls=%fused_computation | convolution fusion | flops 1610612736 | bytes 12845056 | tf_op jit(solution)/shard_map/gnpi,gnqj->npiqj/dot_general | solution.py:27
  307.0 0.1 fusion.3
  307.1 0.2 copy.21
  307.3 0.2 copy.20
  307.4 0.4 fusion.4
  307.9 0.4 fusion.5
  308.3 0.4 fusion
  308.7 0.4 fusion.1
  309.1 0.7 maximum_multiply_fusion
  309.9 0.0 all-reduce.2.cloned.1.call-update
  309.9 124.9 %all-reduce.2.cloned.1.call-done = f32[2,8,32,32]{3,1,2,0:T(8,128)} async-done(((f32[2,8,32,32]{3,1,2,0:T(8,128)}), f32[2,8,32,32]{3,1,2,0:T(8,128)}) %all-reduce.2.cloned.1.call-update) | async-done | bytes 65552 | tf_op jit(solution)/shard_map/psum | solution.py:55
  434.8 1.7 copy.24
  (12 shorter events, 0.0 us)
Async XLA Ops:
  6.5 8.1 %copy-start.1 = (f32[256]{0:T(256)S(1)}, f32[256]{0:T(256)}, u32[]{:S(2)}) copy-start(f32[256]{0:T(256)} %param.8) | copy-start | bytes 3076
  6.5 8.1 %copy-start.2 = (s32[256]{0:T(256)S(1)}, s32[256]{0:T(256)}, u32[]{:S(2)}) copy-start(s32[256]{0:T(256)} %param.11) | copy-start | bytes 3076
  6.5 8.2 %copy-start.3 = (s32[32]{0:T(128)S(1)}, s32[32]{0:T(128)}, u32[]{:S(2)}) copy-start(s32[32]{0:T(128)} %param.10) | copy-start | bytes 388
  6.5 8.4 %copy-start.4 = (f32[8]{0:T(128)S(1)}, f32[8]{0:T(128)}, u32[]{:S(2)}) copy-start(f32[8]{0:T(128)} %param.9) | copy-start | bytes 100
  6.5 25.0 %all-gather.5.cloned.1.call-start = ((), (), s32[]{:S(2)}) async-start(), calls=%async_computation.1 | async-start | bytes 12582912 | tf_op jit(solution)/shard_map/all_gather | solution.py:44
  7.3 262.8 %all-gather.3.cloned.1.call-start = ((), (), s32[]{:S(2)}) async-start(), calls=%async_computation | async-start | bytes 17825792 | tf_op jit(solution)/shard_map/all_gather | solution.py:46
  8.0 426.8 %all-reduce.2.cloned.1.call-start = ((), (), s32[]{:S(2)}) async-start(), calls=%async_computation.2 | async-start | bytes 524288 | tf_op jit(solution)/shard_map/psum | solution.py:55
  270.0 24.3 %copy-start = (bf16[2048,1024]{0,1:T(8,128)(2,1)S(1)}, bf16[2048,1024]{0,1:T(8,128)(2,1)}, u32[]{:S(2)}) copy-start(bf16[2048,1024]{0,1:T(8,128)(2,1)} %copy.19) | copy-start | bytes 12582916
Sparse Core Ops, SparseCore 0:
  8.9 22.5 all-gather.4
  34.2 235.7 all-gather.2
  310.0 124.7 all-reduce.1
where the time goes:
time: 443 us
  waiting for transfers between devices  381 us (86%)
  matrix products  38.6 us (9%)
  between operations  13.2 us (3%)
  local copies, waits for them, and re-layouts  8.72 us (2%)
    all_gather x1, waiting for transfers between devices, shards(): lax.all_gather(screening, 'blk', axis=1, tiled=True)  239 us
    psum x1, waiting for transfers between devices, shards(): return lax.psum(partial_value, ('blk', 'ga'))  125 us
    dot_general x1, matrix products, shards(): jnp.dot(lax.all_gather(screening, 'blk', axis=1, tiled=True), gathered, p...  24.3 us
    all_gather x1, waiting for transfers between devices, shards(): gathered = lax.all_gather(pair_elements, 'ga', axis=0, tiled=True)  16.5 us
    dot_general x1, matrix products, window_sigma(): jnp.einsum('gnpi,gnqj->npiqj', local_elems, image_cols, precision=lax.Pre...  12.7 us
  transfers between devices with their start and end apart: 3, of which 3 were waited for; matrix products, arithmetic and copies ran while one was open for 2% of the time, Pallas kernels for 0%

commit v1 on v0

--- a/solution.py
+++ b/solution.py
@@ -5,6 +5,12 @@
 
 STATES = 32
 NG = 4096
+
+
+def add_all(x, mesh_axis):
+    blocks = lax.all_gather(x, mesh_axis, axis=0, tiled=False)
+    total = blocks.sum(axis=0)
+    return total
 
 
 def band_weights(energies, frequencies, qp_index, occupied, offset, band_count):
@@ -52,7 +58,7 @@
         energies, frequencies, qp_index, occupied, band_start, band_count
     )
     partial_value = window_sigma(pair_elements, screened, weight_real, weight_imag, band_count)
-    return lax.psum(partial_value, ("blk", "ga"))
+    return add_all(partial_value, ("blk", "ga"))
 
 
 def solution(mesh):

time: 443 us -> 397 us (0.90)
  waiting for transfers between devices: 381 us -> 332 us
  other arithmetic: 1.07 us -> 5.53 us
    psum x1 -> x0, waiting for transfers between devices: 125 us -> none  [shards(): return lax.psum(partial_value, ('blk', 'ga'))]
    all_gather x0 -> x1, waiting for transfers between devices: none -> 75.4 us  [add_all(): blocks = lax.all_gather(x, mesh_axis, axis=0, tiled=False)]
    reduce_sum x0 -> x1, other arithmetic: none -> 5.16 us  [add_all(): total = blocks.sum(axis=0)]
where the time goes in v1:
time: 397 us
  waiting for transfers between devices  332 us (84%)
  matrix products  38.6 us (10%)
  between operations  13.2 us (3%)
  local copies, waits for them, and re-layouts  7.77 us (2%)
  other arithmetic  5.53 us (1%)
    all_gather x1, waiting for transfers between devices, shards(): lax.all_gather(screening, 'blk', axis=1, tiled=True)  239 us
    all_gather x1, waiting for transfers between devices, add_all(): blocks = lax.all_gather(x, mesh_axis, axis=0, tiled=False)  75.4 us
    dot_general x1, matrix products, shards(): jnp.dot(lax.all_gather(screening, 'blk', axis=1, tiled=True), gathered, p...  24.3 us
    all_gather x1, waiting for transfers between devices, shards(): gathered = lax.all_gather(pair_elements, 'ga', axis=0, tiled=True)  16.5 us
    dot_general x1, matrix products, window_sigma(): jnp.einsum('gnpi,gnqj->npiqj', local_elems, image_cols, precision=lax.Pre...  12.7 us
  transfers between devices with their start and end apart: 3, of which 3 were waited for; matrix products, arithmetic and copies ran while one was open for 2% of the time, Pallas kernels for 0%

profile of v1, /device:TPU:0, one launch (start us, length us, event | category | flops | bytes accessed | tf_op | source)
XLA Modules:
  0.0 397.0 jit_solution(14370914172628497186)
XLA Ops:
  6.5 0.0 all-gather.6.cloned.1.call-start
  6.6 0.7 all-gather.6.cloned.1.call-update
  7.3 0.0 all-gather.4.cloned.1.call-start
  7.3 0.7 all-gather.4.cloned.1.call-update
  8.0 0.0 all-gather.8.cloned.1.call-start
  8.1 6.6 %copy.25 = bf16[2048,1024]{0,1:T(8,128)(2,1)} copy(bf16[2048,1024]{1,0:T(8,128)(2,1)} %param.6) | data formatting | bytes 8388608 | tf_op args[0]
  14.7 0.1 dynamic_slice.3
  14.8 0.2 select_reduce_fusion
  14.9 0.1 broadcast_subtract_fusion
  15.0 16.5 %all-gather.6.cloned.1.call-done = bf16[4096,1024]{1,0:T(8,128)(2,1)} async-done(((bf16[2048,1024]{1,0:T(8,128)(2,1)}), bf16[4096,1024]{1,0:T(8,128)(2,1)}) %all-gather.6.cloned.1.call-update) | async-done | bytes 8388624 | tf_op jit(solution)/shard_map/all_gather | solution.py:50
  31.5 238.5 %all-gather.4.cloned.1.call-done = bf16[2048,4096]{1,0:T(8,128)(2,1)} async-done(((bf16[2048,256]{1,0:T(8,128)(2,1)}), bf16[2048,4096]{1,0:T(8,128)(2,1)}) %all-gather.4.cloned.1.call-update) | async-done | bytes 16777232 | tf_op jit(solution)/shard_map/all_gather | solution.py:52
  270.0 24.3 %fusion.20 = f32[2048,1024]{0,1:T(8,128)} fusion(bf16[2048,4096]{1,0:T(8,128)(2,1)} %all-gather.4.cloned.1.call-done, bf16[4096,1024]{1,0:T(8,128)(2,1)} %all-gather.6.cloned.1.call-done), kind=kOutput, calls=%fused_computation.32 | convolution fusion | flops 17179869184 | bytes 33554432 | tf_op jit(solution)/shard_map/dot_general | solution.py:51
  294.3 12.7 %convolution_bitcast_fusion = f32[16,2,32,2,32]{2,4,1,3,0:T(8,128)S(1)} fusion(f32[2048,16,2,32,1]{0,3,4,2,1:T(8,128)} %bitcast.33, bf16[2048,16,2,32,1]{0,3,2,4,1:T(8,128)(2,1)S(1)} %bitcast.32), kind=kOutput, calls=%fused_computation | convolution fusion | flops 1610612736 | bytes 12845056 | tf_op jit(solution)/shard_map/gnpi,gnqj->npiqj/dot_general | solution.py:33
  307.0 0.1 fusion.3
  307.1 0.2 copy.27
  307.3 0.2 copy.26
  307.4 0.4 fusion.4
  307.9 0.4 fusion.5
  308.3 0.4 fusion
  308.7 0.4 fusion.1
  309.2 0.8 copy.30
  309.9 0.0 all-gather.8.cloned.1.call-update
  309.9 75.4 %all-gather.8.cloned.1.call-done = f32[32,2,8,32,32]{4,3,2,1,0:T(8,128)} async-done(((f32[1,2,8,32,32]{4,3,2,1,0:T(8,128)}), f32[32,2,8,32,32]{4,3,2,1,0:T(8,128)}) %all-gather.8.cloned.1.call-update) | async-done | bytes 2097168 | tf_op jit(solution)/shard_map/all_gather | solution.py:11
  385.3 5.2 %reduce_sum.19 = f32[2,8,32,32]{3,2,1,0:T(8,128)} reduce(f32[32,2,8,32,32]{4,3,2,1,0:T(8,128)} %all-gather.8.cloned.1.call-done, f32[]{:T(128)} %constant.5.clone.1), dimensions={0}, to_apply=%region_1.2 | reduce | flops 507904 | bytes 2162692 | tf_op jit(solution)/shard_map/reduce_sum | solution.py:12
  (13 shorter events, 0.1 us)
Async XLA Ops:
  6.5 8.1 %copy-start.1 = (f32[256]{0:T(256)S(1)}, f32[256]{0:T(256)}, u32[]{:S(2)}) copy-start(f32[256]{0:T(256)} %param.8) | copy-start | bytes 3076
  6.5 8.1 %copy-start.2 = (s32[256]{0:T(256)S(1)}, s32[256]{0:T(256)}, u32[]{:S(2)}) copy-start(s32[256]{0:T(256)} %param.11) | copy-start | bytes 3076
  6.5 8.2 %copy-start.3 = (s32[32]{0:T(128)S(1)}, s32[32]{0:T(128)}, u32[]{:S(2)}) copy-start(s32[32]{0:T(128)} %param.10) | copy-start | bytes 388
  6.5 8.4 %copy-start.4 = (f32[8]{0:T(128)S(1)}, f32[8]{0:T(128)}, u32[]{:S(2)}) copy-start(f32[8]{0:T(128)} %param.9) | copy-start | bytes 100
  6.5 25.0 %all-gather.6.cloned.1.call-start = ((), (), s32[]{:S(2)}) async-start(), calls=%async_computation.1 | async-start | bytes 12582912 | tf_op jit(solution)/shard_map/all_gather | solution.py:50
  7.3 262.8 %all-gather.4.cloned.1.call-start = ((), (), s32[]{:S(2)}) async-start(), calls=%async_computation | async-start | bytes 17825792 | tf_op jit(solution)/shard_map/all_gather | solution.py:52
  8.0 377.3 %all-gather.8.cloned.1.call-start = ((), (), s32[]{:S(2)}) async-start(), calls=%async_computation.2 | async-start | bytes 8650752 | tf_op jit(solution)/shard_map/all_gather | solution.py:11
  270.0 24.3 %copy-start = (bf16[2048,1024]{0,1:T(8,128)(2,1)S(1)}, bf16[2048,1024]{0,1:T(8,128)(2,1)}, u32[]{:S(2)}) copy-start(bf16[2048,1024]{0,1:T(8,128)(2,1)} %copy.25) | copy-start | bytes 12582916
Sparse Core Ops, SparseCore 0:
  8.9 22.5 all-gather.5
  34.2 235.7 all-gather.3
  310.1 75.2 all-gather.7
